TPU v7x, 32 devices: a whole 2x2x4 slice. The times are simulated.
32 devices in a mesh: row: 4 (over y, core), col: 8 (over z, x).
Axes of the slice: x: 2, y: 2, z: 4, core: 2. Of those that a mesh axis runs over, the one named last changes fastest.
Arguments:
- l_saved: bfloat16 [16, 4, 256, 8, 256], P(None, 'row', None, 'col'), as said below
- l_grad: bfloat16 [16, 4, 256, 8, 256], P(None, 'row', None, 'col'), as said below
Outputs:
- grad_out: float32 [16, 4, 256, 8, 256], P(None, 'row', None, 'col')
Inputs may be any that keep to these rules, and one draw needn't show every extreme that they name: Read as one matrix of 16384 rows, l_saved is lower triangular with its diagonal between 1 and 2. Read as one matrix, l_grad is zero above the diagonal.
All inputs are finite; a program needn't handle non-finite values.
Results may differ from a plain program's by a relative error of at most 0.0003.
Values may be sent and summed in bfloat16 or wider, within the bound.
A program may use at most 64 MiB of HBM per device.

v0:
```python
import jax
import jax.numpy as jnp
from jax import lax
from jax.sharding import PartitionSpec as P

F32 = jnp.float32
BF16 = jnp.bfloat16
HIGH3 = lax.Precision.HIGH


def dot3(a, b, ca=1, cb=0):
    return lax.dot_general(
        a, b, (((ca,), (cb,)), ((), ())), precision=HIGH3, preferred_element_type=F32
    )


def bdot(a, b):
    return lax.dot_general(
        a, b, (((2,), (1,)), ((0,), (0,))), precision=HIGH3, preferred_element_type=F32
    )


def inverse_pair(tiles):
    tile = tiles.shape[-1]
    rows = lax.broadcasted_iota(jnp.int32, (tile, tile), 0)
    cols = lax.broadcasted_iota(jnp.int32, (tile, tile), 1)
    eye = (rows == cols).astype(F32)
    recip = 1.0 / jnp.sum(tiles * eye, axis=2)
    inv = eye * recip[:, None, :]
    size = 1
    while size < tile:
        off = (rows // size % 2 == 1) & (cols // size == rows // size - 1)
        part = jnp.where(off, tiles, 0.0)
        if size == 1:
            inv = inv - recip[:, :, None] * part * recip[:, None, :]
        else:
            inv = inv - bdot(inv, bdot(part, inv))
        size *= 2
    return inv


def per_device(l_saved, l_grad):
    rows_here, tile = (l_saved.shape[0], l_saved.shape[2])
    n_row = lax.axis_size("row")
    n_col = lax.axis_size("col")
    factor = l_saved.reshape(rows_here, tile, tile)
    grad = l_grad.reshape(rows_here, tile, tile)
    my_row = lax.axis_index("row")
    my_col = lax.axis_index("col")
    assert n_col % n_row == 0
    first = n_col // n_row
    loc = first - 1
    lo, hi = (n_col - 2, n_col - 1)
    l_dk = lax.all_gather(factor[loc], "row")[n_row - 2 :].reshape(2 * tile, tile)
    mine = jnp.concatenate([l_dk, grad[first:].reshape(-1, tile)], 0)
    zero = jnp.zeros_like(mine)
    both = jnp.concatenate(
        [jnp.where(my_col == lo, mine, zero), jnp.where(my_col == hi, mine, zero)], 1
    )
    both = lax.psum(both, "col")
    l_dd = both[: 2 * tile].astype(F32)
    g_d = both[2 * tile :]
    l66, l76, l77 = (l_dd[:tile, :tile], l_dd[tile:, :tile], l_dd[tile:, tile:])
    inv = inverse_pair(jnp.stack([l66, l77]))
    w76 = -dot3(inv[1], dot3(l76, inv[0]))
    w = jnp.concatenate(
        [jnp.concatenate([inv[0], jnp.zeros_like(w76)], 1), jnp.concatenate([w76, inv[1]], 1)], 0
    )
    below_l = factor[first:].reshape(-1, tile)
    h = lax.dot_general(g_d, below_l, (((0,), (0,)), ((), ())), preferred_element_type=F32)
    t = dot3(w, lax.psum(h, "row"), 0, 0)
    fresh = grad[loc].astype(F32)
    g_dk = lax.all_gather(grad[loc], "row")[n_row - 2 :].reshape(2 * tile, tile).astype(F32)
    q_mine = g_dk - t
    z2 = jnp.zeros_like(q_mine)
    q = lax.psum(
        jnp.concatenate(
            [jnp.where(my_col == lo, q_mine, z2), jnp.where(my_col == hi, q_mine, z2)], 1
        ),
        "col",
    )
    eye2 = jnp.eye(2 * tile, dtype=F32)
    q = jnp.tril(q)
    m = dot3(l_dd, q, 0, 0)
    phi = jnp.tril(m) - 0.5 * m * eye2
    half = dot3(dot3(w, phi, 0, 0), w)
    s = half + half.T
    out_dd = jnp.tril(s) - 0.5 * s * eye2
    right = my_col >= lo
    w_mine = jnp.where(my_col == lo, w[:, :tile], w[:, tile:])
    x = jnp.where(right, -w_mine, dot3(w, l_dk.astype(F32)))
    x_hi = lax.reduce_precision(x, 8, 7)
    x_lo = (x - x_hi).astype(BF16)
    x_hi = x_hi.astype(BF16)
    prod = jnp.dot(g_d, x_hi, preferred_element_type=F32) + jnp.dot(
        g_d, x_lo, preferred_element_type=F32
    )
    base = jnp.where(right, jnp.zeros((), BF16), grad[first:]).astype(F32)
    low = base - prod.reshape(-1, tile, tile)
    at_lo = my_row == n_row - 2
    s_row = jnp.where(at_lo, s[:tile], s[tile:])
    t_row = jnp.where(at_lo, t[:tile], t[tile:])
    own = fresh - (t_row + dot3(s_row, l_dk.astype(F32)))
    d_row = jnp.where(at_lo, out_dd[:tile], out_dd[tile:])
    d_own = jnp.where(my_col == lo, d_row[:, :tile], d_row[:, tile:])
    in_panel = my_row >= n_row - 2
    zt = jnp.zeros_like(fresh)
    own = jnp.where(in_panel, jnp.where(right, d_own, own), jnp.where(right, zt, fresh))
    upper = jnp.where(right, jnp.zeros((), BF16), grad[:loc]).astype(F32)
    out = jnp.concatenate([upper, own[None], low], 0)
    return out.reshape(l_grad.shape)


def solution(mesh):
    spec = P(None, "row", None, "col", None)
    return jax.shard_map(
        per_device, mesh=mesh, in_specs=(spec, spec), out_specs=spec, check_vma=False
    )
```

profile of v0, /device:TPU:0, one launch (start us, length us, event | category | flops | bytes accessed | tf_op | source)
XLA Modules:
  0.0 323.6 jit_solution(8879946724786427271)
XLA Ops:
  6.5 0.9 slice.87
  7.5 8.7 %all-gather = bf16[4,1,256,1,256]{4,2,3,1,0:T(8,128)(2,1)S(1)} all-gather(bf16[1,1,256,1,256]{4,2,3,1,0:T(8,128)(2,1)S(1)} %slice.87), channel_id=2, replica_groups=mesh['row'=4,'col'=8] {'row'}, dimensions={0}, use_global_device_ids=true | all-gather | bytes 655360 | tf_op jit(solution)/shard_map/all_gather | solution.py:54
  16.2 1.7 slice.115
  17.9 0.7 broadcast_select_fusion.1
  18.6 2.3 pad_maximum_fusion
  21.0 1.5 copy-done.3
  22.5 0.7 bitcast_convert_fusion
  23.2 7.3 %all-gather.1 = bf16[4,1,256,1,256]{4,2,3,1,0:T(8,128)(2,1)S(1)} all-gather(bf16[1,1,256,1,256]{4,2,3,1,0:T(8,128)(2,1)S(1)} %get-tuple-element.8), channel_id=3, replica_groups=mesh['row'=4,'col'=8] {'row'}, dimensions={0}, use_global_device_ids=true | all-gather | bytes 655360 | tf_op jit(solution)/shard_map/all_gather | solution.py:73
  30.5 0.7 slice.122
  32.9 145.4 %all-reduce.5.cloned.1.call-done = bf16[4096,512]{1,0:T(8,128)(2,1)} async-done(((bf16[4096,512]{1,0:T(8,128)(2,1)}), bf16[4096,512]{1,0:T(8,128)(2,1)}) %all-reduce.5.cloned.1.call-update) | async-done | bytes 4194320 | tf_op jit(solution)/shard_map/psum | solution.py:60
  178.3 1.2 slice_convert_fusion
  179.7 0.5 fusion.34
  180.2 0.5 convolution_subtract_fusion.6
  180.7 0.4 fusion.32
  182.3 0.4 fusion.28
  185.6 0.5 copy-done
  186.8 1.9 fusion.3
  189.1 1.4 convolution_select_fusion
  190.5 30.8 %all-reduce.7.cloned.1.call-done = f32[512,256]{1,0:T(8,128)} async-done(((f32[512,256]{1,0:T(8,128)}), f32[512,256]{1,0:T(8,128)}) %all-reduce.7.cloned.1.call-update) | async-done | bytes 524304 | tf_op jit(solution)/shard_map/psum | solution.py:71
  221.3 2.7 fusion.40
  224.0 1.2 pad_maximum_fusion.3
  225.2 3.3 %fusion.1 = f32[3584,256]{1,0:T(8,128)S(1)} fusion(bf16[4096,512]{1,0:T(8,128)(2,1)} %all-reduce.5.cloned.1.call-done, f32[512,256]{1,0:T(8,128)S(1)} %convolution_select_fusion), kind=kOutput, calls=%fused_computation.5 | convolution fusion | flops 939786240 | bytes 7864320 | tf_op jit(solution)/shard_map/dot_general | solution.py:95
  228.5 1.1 convolution_add_fusion
  229.7 2.3 convert_subtract_fusion
  231.9 71.8 %all-reduce.9.cloned.1.call-done = f32[512,512]{1,0:T(8,128)} async-done(((f32[512,512]{1,0:T(8,128)}), f32[512,512]{1,0:T(8,128)}) %all-reduce.9.cloned.1.call-update) | async-done | bytes 1048592 | tf_op jit(solution)/shard_map/psum | solution.py:76
  303.7 2.2 fusion.14
  305.9 1.0 fusion.9
  307.0 2.0 fusion.113
  309.0 1.3 copy.12
  310.3 1.6 select_subtract_fusion
  312.4 0.5 copy-done.2
  313.2 3.9 %reshape.79 = f32[16,1,256,1,256]{4,3,2,1,0:T(1,128)} reshape(f32[16,256,256]{2,1,0:T(8,128)S(1)} %pad_maximum_fusion.1) | data formatting | bytes 8388608 | tf_op jit(solution)/shard_map/reshape | solution.py:111
  (69 shorter events, 7.6 us)
Async XLA Ops:
  6.5 171.8 %all-reduce.5.cloned.1.call-start = ((), (), s32[]{:S(2)}) async-start(), calls=%async_computation | async-start | bytes 8388608 | tf_op jit(solution)/shard_map/psum | solution.py:60
  16.2 2.4 copy-start.6
  20.9 1.6 copy-start.3
  20.9 200.4 %all-reduce.7.cloned.1.call-start = ((), (), s32[]{:S(2)}) async-start(), calls=%async_computation.1 | async-start | bytes 1048576 | tf_op jit(solution)/shard_map/psum | solution.py:71
  183.9 2.2 copy-start
  184.3 2.5 slice-start
  186.1 119.8 %copy-start.4 = (f32[256,256]{1,0:T(8,128)}, f32[256,256]{1,0:T(8,128)S(1)}, u32[]{:S(2)}) copy-start(f32[256,256]{1,0:T(8,128)S(1)} %get-tuple-element.15) | copy-start | bytes 786436
  186.1 119.8 %copy-start.5 = (f32[256,256]{1,0:T(8,128)}, f32[256,256]{1,0:T(8,128)S(1)}, u32[]{:S(2)}) copy-start(f32[256,256]{1,0:T(8,128)S(1)} %get-tuple-element.16) | copy-start | bytes 786436
  188.8 115.0 %all-reduce.9.cloned.1.call-start = ((), (), s32[]{:S(2)}) async-start(), calls=%async_computation.2 | async-start | bytes 2097152 | tf_op jit(solution)/shard_map/psum | solution.py:76
  225.2 3.3 %copy-start.1 = (bf16[4096,512]{1,0:T(8,128)(2,1)S(1)}, bf16[4096,512]{1,0:T(8,128)(2,1)}, u32[]{:S(2)}) copy-start(bf16[4096,512]{1,0:T(8,128)(2,1)} %all-reduce.5.cloned.1.call-done) | copy-start | bytes 12582916
  309.0 3.1 copy-start.7
  310.3 1.7 copy-start.9
  310.3 2.5 copy-start.2
  310.3 2.5 copy-start.8
Sparse Core Ops, SparseCore 0:
  21.1 157.1 all-reduce.4
  188.9 32.3 all-reduce.6
  225.3 78.3 all-reduce.8
where the time goes:
time: 324 us
  waiting for transfers between devices  248 us (77%)
  matrix products  22.3 us (7%)
  blocking collectives  15.9 us (5%)
  between operations  13.6 us (4%)
  other arithmetic  12.1 us (4%)
  local copies, waits for them, and re-layouts  11.3 us (3%)
    psum x1, waiting for transfers between devices, per_device(): both = lax.psum(both, 'col')  145 us
    psum x1, waiting for transfers between devices, per_device(): lax.psum(jnp.concatenate([jnp.where(my_col == lo, q_mine, z2), jnp.where(...  71.8 us
    psum x1, waiting for transfers between devices, per_device(): t = dot3(w, lax.psum(h, 'row'), 0, 0)  30.8 us
    dot_general x8, matrix products, dot3(): lax.dot_general(a, b, (((ca,), (cb,)), ((), ())), precision=HIGH3, prefer...  10.1 us
    all_gather x1, blocking collectives, per_device(): lax.all_gather(factor[loc], 'row')[n_row - 2:].reshape(2 * tile, tile)  8.68 us
    all_gather x1, blocking collectives, per_device(): lax.all_gather(grad[loc], 'row')[n_row - 2:].reshape(2 * tile, tile)  7.26 us
  transfers between devices with their start and end apart: 3, of which 3 were waited for; matrix products, arithmetic and copies ran while one was open for 3% of the time, Pallas kernels for 0%

commit v1 on v0

--- a/solution.py
+++ b/solution.py
@@ -68,7 +68,7 @@
     )
     below_l = factor[first:].reshape(-1, tile)
     h = lax.dot_general(g_d, below_l, (((0,), (0,)), ((), ())), preferred_element_type=F32)
-    t = dot3(w, lax.psum(h, "row"), 0, 0)
+    t = dot3(w, jnp.sum(lax.all_gather(h, "row"), axis=0), 0, 0)
     fresh = grad[loc].astype(F32)
     g_dk = lax.all_gather(grad[loc], "row")[n_row - 2 :].reshape(2 * tile, tile).astype(F32)
     q_mine = g_dk - t

time: 324 us -> 312 us (0.963)
  waiting for transfers between devices: 248 us -> 233 us
    psum x1 -> x0, waiting for transfers between devices: 30.8 us -> none  [per_device(): t = dot3(w, lax.psum(h, 'row'), 0, 0)]
    all_gather x0 -> x1, waiting for transfers between devices: none -> 16.2 us  [per_device(): t = dot3(w, jnp.sum(lax.all_gather(h, 'row'), axis=0), 0, 0)]
  transfers between devices with their start and end apart: 3 -> 3, of which waited for: 3 -> 3; matrix products, arithmetic and copies ran while one was open for 3% -> 5% of each run, Pallas kernels for 0% -> 0%
where the time goes in v1:
time: 312 us
  waiting for transfers between devices  233 us (75%)
  matrix products  22.2 us (7%)
  blocking collectives  15.9 us (5%)
  other arithmetic  14.7 us (5%)
  between operations  13.6 us (4%)
  local copies, waits for them, and re-layouts  11.8 us (4%)
    psum x1, waiting for transfers between devices, per_device(): both = lax.psum(both, 'col')  145 us
    psum x1, waiting for transfers between devices, per_device(): lax.psum(jnp.concatenate([jnp.where(my_col == lo, q_mine, z2), jnp.where(...  71.7 us
    all_gather x1, waiting for transfers between devices, per_device(): t = dot3(w, jnp.sum(lax.all_gather(h, 'row'), axis=0), 0, 0)  16.2 us
    dot_general x8, matrix products, dot3(): lax.dot_general(a, b, (((ca,), (cb,)), ((), ())), precision=HIGH3, prefer...  10.1 us
    all_gather x1, blocking collectives, per_device(): lax.all_gather(factor[loc], 'row')[n_row - 2:].reshape(2 * tile, tile)  8.68 us
    all_gather x1, blocking collectives, per_device(): lax.all_gather(grad[loc], 'row')[n_row - 2:].reshape(2 * tile, tile)  7.26 us
  transfers between devices with their start and end apart: 3, of which 3 were waited for; matrix products, arithmetic and copies ran while one was open for 5% of the time, Pallas kernels for 0%

profile of v1, /device:TPU:0, one launch (start us, length us, event | category | flops | bytes accessed | tf_op | source)
XLA Modules:
  0.0 311.9 jit_solution(2861691578025098001)
XLA Ops:
  6.5 0.9 slice.87
  7.5 8.7 %all-gather = bf16[4,1,256,1,256]{4,2,3,1,0:T(8,128)(2,1)S(1)} all-gather(bf16[1,1,256,1,256]{4,2,3,1,0:T(8,128)(2,1)S(1)} %slice.87), channel_id=2, replica_groups=mesh['row'=4,'col'=8] {'row'}, dimensions={0}, use_global_device_ids=true | all-gather | bytes 655360 | tf_op jit(solution)/shard_map/all_gather | solution.py:54
  16.2 1.7 slice.115
  17.9 0.7 broadcast_select_fusion.1
  18.6 2.3 pad_maximum_fusion
  21.0 1.5 copy-done.3
  22.5 0.7 bitcast_convert_fusion
  23.2 7.3 %all-gather.1 = bf16[4,1,256,1,256]{4,2,3,1,0:T(8,128)(2,1)S(1)} all-gather(bf16[1,1,256,1,256]{4,2,3,1,0:T(8,128)(2,1)S(1)} %get-tuple-element.8), channel_id=3, replica_groups=mesh['row'=4,'col'=8] {'row'}, dimensions={0}, use_global_device_ids=true | all-gather | bytes 655360 | tf_op jit(solution)/shard_map/all_gather | solution.py:73
  30.5 0.8 slice.122
  32.9 145.4 %all-reduce.4.cloned.1.call-done = bf16[4096,512]{1,0:T(8,128)(2,1)} async-done(((bf16[4096,512]{1,0:T(8,128)(2,1)}), bf16[4096,512]{1,0:T(8,128)(2,1)}) %all-reduce.4.cloned.1.call-update) | async-done | bytes 4194320 | tf_op jit(solution)/shard_map/psum | solution.py:60
  178.3 1.2 slice_convert_fusion
  179.7 0.5 fusion.34
  180.2 0.5 convolution_subtract_fusion.6
  182.3 0.6 copy-done
  182.9 0.6 slice-done
  183.5 1.9 fusion.3
  188.9 1.1 fusion.99
  191.0 16.2 %all-gather.5.cloned.1.call-done = f32[2048,256]{1,0:T(8,128)} async-done(((f32[512,256]{1,0:T(8,128)}), f32[2048,256]{1,0:T(8,128)}) %all-gather.5.cloned.1.call-update) | async-done | bytes 2097168 | tf_op jit(solution)/shard_map/all_gather | solution.py:71
  207.1 2.6 reduce_sum.19
  209.7 2.7 fusion.40
  212.4 1.1 pad_maximum_fusion.3
  213.6 3.3 %fusion.1 = f32[3584,256]{1,0:T(8,128)S(1)} fusion(bf16[4096,512]{1,0:T(8,128)(2,1)} %all-reduce.4.cloned.1.call-done, f32[512,256]{1,0:T(8,128)S(1)} %convolution_select_fusion), kind=kOutput, calls=%fused_computation.5 | convolution fusion | flops 939786240 | bytes 7864320 | tf_op jit(solution)/shard_map/dot_general | solution.py:95
  216.9 1.1 convolution_add_fusion
  218.1 2.3 convert_subtract_fusion
  220.3 71.7 %all-reduce.6.cloned.1.call-done = f32[512,512]{1,0:T(8,128)} async-done(((f32[512,512]{1,0:T(8,128)}), f32[512,512]{1,0:T(8,128)}) %all-reduce.6.cloned.1.call-update) | async-done | bytes 1048592 | tf_op jit(solution)/shard_map/psum | solution.py:76
  292.0 2.2 fusion.14
  294.2 1.0 fusion.9
  295.3 2.0 fusion.113
  297.3 1.3 copy.12
  298.6 1.6 select_subtract_fusion
  300.7 0.4 copy-done.2
  301.5 3.9 %reshape.79 = f32[16,1,256,1,256]{4,3,2,1,0:T(1,128)} reshape(f32[16,256,256]{2,1,0:T(8,128)S(1)} %pad_maximum_fusion.1) | data formatting | bytes 8388608 | tf_op jit(solution)/shard_map/reshape | solution.py:111
  (72 shorter events, 8.5 us)
Async XLA Ops:
  6.5 171.8 %all-reduce.4.cloned.1.call-start = ((), (), s32[]{:S(2)}) async-start(), calls=%async_computation | async-start | bytes 8388608 | tf_op jit(solution)/shard_map/psum | solution.py:60
  16.2 2.4 copy-start.6
  20.9 1.6 copy-start.3
  20.9 186.2 %all-gather.5.cloned.1.call-start = ((), (), s32[]{:S(2)}) async-start(), calls=%async_computation.2 | async-start | bytes 2621440 | tf_op jit(solution)/shard_map/all_gather | solution.py:71
  180.7 2.2 copy-start
  180.7 2.8 slice-start
  185.4 106.6 %all-reduce.6.cloned.1.call-start = ((), (), s32[]{:S(2)}) async-start(), calls=%async_computation.1 | async-start | bytes 2097152 | tf_op jit(solution)/shard_map/psum | solution.py:76
  188.1 2.4 copy-start.7
  190.1 104.1 %copy-start.4 = (f32[256,256]{1,0:T(8,128)}, f32[256,256]{1,0:T(8,128)S(1)}, u32[]{:S(2)}) copy-start(f32[256,256]{1,0:T(8,128)S(1)} %get-tuple-element.15) | copy-start | bytes 786436
  190.1 104.1 %copy-start.5 = (f32[256,256]{1,0:T(8,128)}, f32[256,256]{1,0:T(8,128)S(1)}, u32[]{:S(2)}) copy-start(f32[256,256]{1,0:T(8,128)S(1)} %get-tuple-element.16) | copy-start | bytes 786436
  213.6 3.3 %copy-start.1 = (bf16[4096,512]{1,0:T(8,128)(2,1)S(1)}, bf16[4096,512]{1,0:T(8,128)(2,1)}, u32[]{:S(2)}) copy-start(bf16[4096,512]{1,0:T(8,128)(2,1)} %all-reduce.4.cloned.1.call-done) | copy-start | bytes 12582916
  297.2 3.1 copy-start.8
  298.6 1.7 copy-start.10
  298.6 2.5 copy-start.2
  298.6 2.5 copy-start.9
Sparse Core Ops, SparseCore 0:
  21.1 157.1 all-reduce.3
  185.6 21.5 all-gather.4
  213.7 78.2 all-reduce.5
